TPU v7x, 128 devices: a whole 4x4x4 slice. The times are simulated.
128 devices in a mesh: pts: 128 (over z, y, x, core).
Axes of the slice: x: 4, y: 4, z: 4, core: 2. Of those that a mesh axis runs over, the one named last changes fastest.
Arguments:
- points: bfloat16 [65536, 64], P('pts'), may hold values from -10 to 10, as said below
- targets: float32 [65536], P('pts'), may hold values from -6 to 6
- ridge_weight: float32 [], replicated, may hold values from 0.5 to 4
Outputs:
- coefficients: float32 [65536], P('pts')
- residual: float32 [65536], P('pts')
Inputs may be any that keep to these rules, and one draw needn't show every extreme that they name: `points`: each point lies near one of 1365 cluster centres; every coordinate is within -10 and 10.
All inputs are finite; a program needn't handle non-finite values.
Results may differ from a plain program's by a relative error of at most 0.005.
Values may be sent and summed in bfloat16 or wider, within the bound.
A program may use at most 192 MiB of HBM per device.

v0:
```python
import jax
import jax.numpy as jnp
from jax import lax
from jax.sharding import PartitionSpec as P

ITERS = 2


def over_all(shard, axis, dim, absorb, state):
    everything = jax.tree.map(lambda a: lax.all_gather(a, axis, axis=dim, tiled=True), shard)
    return absorb(state, everything, jnp.int32(0))


def kernel_times(own_points, own_norms, shard_rows, coef_part, inverse_width):
    widened = shard_rows.astype(jnp.float32)
    shard_norms = jnp.sum(widened * widened, axis=1)
    cross_term = jnp.dot(own_points, shard_rows.T, preferred_element_type=jnp.float32)
    distance = own_norms[:, None] + shard_norms[None, :] - 2.0 * cross_term
    kernel = jnp.exp(-inverse_width * distance).astype(jnp.bfloat16)
    return jnp.dot(kernel, coef_part, preferred_element_type=jnp.float32)


def apply_operator(direction, points, own_norms, ridge_weight, inverse_width):
    coef_whole = lax.all_gather(direction, "pts", axis=0, tiled=True).astype(jnp.bfloat16)
    local_rows = points.shape[0]
    empty = jnp.zeros((local_rows,), jnp.float32)

    def accumulate(running, shard_rows, first_row):
        coef_part = lax.dynamic_slice_in_dim(coef_whole, first_row, shard_rows.shape[0], 0)
        return running + kernel_times(points, own_norms, shard_rows, coef_part, inverse_width)

    summed = over_all(points, "pts", 0, accumulate, empty)
    return summed + ridge_weight * direction


def body(points, targets, ridge_weight):
    inverse_width = 1.0 / points.shape[1]
    widened = points.astype(jnp.float32)
    own_norms = jnp.sum(widened * widened, axis=1)
    coefficients = jnp.zeros_like(targets)
    residual = targets
    direction = targets
    norm_now = lax.psum(jnp.sum(residual * residual), "pts")
    for iteration in range(ITERS):
        applied = apply_operator(direction, points, own_norms, ridge_weight, inverse_width)
        curvature = lax.psum(jnp.sum(direction * applied), "pts")
        step_size = norm_now / curvature
        coefficients = coefficients + step_size * direction
        residual = residual - step_size * applied
        if iteration + 1 < ITERS:
            norm_next = lax.psum(jnp.sum(residual * residual), "pts")
            direction = residual + norm_next / norm_now * direction
            norm_now = norm_next
    return (coefficients, residual)


def solution(mesh):
    in_specs = (P("pts", None), P("pts"), P())
    out_specs = (P("pts"), P("pts"))
    return jax.shard_map(body, mesh=mesh, in_specs=in_specs, out_specs=out_specs, check_vma=False)
```

profile of v0, /device:TPU:1, one launch (start us, length us, event | category | flops | bytes accessed | tf_op | source)
XLA Modules:
  0.0 420.6 jit_solution(7637829127541475642)
XLA Ops:
  7.2 0.0 all-gather.4.cloned.1.call-start
  7.2 0.7 all-gather.4.cloned.1.call-update
  7.9 0.7 convert
  9.2 38.9 %all-gather = bf16[128,1,512]{2,1,0:T(2,128)(2,1)S(1)} all-gather(bf16[1,1,512]{2,1,0:T(2,128)(2,1)S(1)} %convert), channel_id=1, replica_groups=mesh['pts'=128] {'pts'}, dimensions={0}, use_global_device_ids=true | all-gather | bytes 132096 | tf_op jit(solution)/shard_map/all_gather | solution.py:24
  48.1 0.9 multiply_reduce_fusion.1
  49.0 38.6 %all-gather.4.cloned.1.call-done = bf16[65536,64]{0,1:T(8,128)(2,1)} async-done(((bf16[512,64]{0,1:T(8,128)(2,1)}), bf16[65536,64]{0,1:T(8,128)(2,1)}) %all-gather.4.cloned.1.call-update) | async-done | bytes 8388624 | tf_op jit(solution)/shard_map/all_gather | solution.py:10
  87.6 5.4 %multiply_reduce_fusion = f32[65536]{0:T(1024)S(1)} fusion(bf16[65536,64]{0,1:T(8,128)(2,1)} %all-gather.4.cloned.1.call-done), kind=kLoop, calls=%fused_computation.1 | loop fusion | flops 12517376 | bytes 8650752 | tf_op jit(solution)/shard_map/reduce_sum | solution.py:16
  93.0 36.6 %exponential_convert_fusion = bf16[512,65536]{1,0:T(8,128)(2,1)} fusion(bf16[512,64]{0,1:T(8,128)(2,1)} %param.3, bf16[65536,64]{0,1:T(8,128)(2,1)} %all-gather.4.cloned.1.call-done, f32[65536]{0:T(1024)S(1)} %multiply_reduce_fusion, f32[512]{0:T(512)S(1)} %multiply_reduce_fusion.1), kind=kOutput, calls=%fused_computation | convolution fusion | flops 4462739456 | bytes 75827200 | tf_op jit(solution)/shard_map/dot_general | solution.py:17
  129.7 0.0 copy-start
  129.7 26.6 %fusion = f32[1,512]{1,0:T(1,128)S(1)} fusion(bf16[512,65536]{1,0:T(8,128)(2,1)} %exponential_convert_fusion, bf16[65536,1]{0,1:T(2,128)(2,1)S(1)} %bitcast.12), kind=kOutput, calls=%fused_computation.13 | convolution fusion | flops 67108864 | bytes 67241984 | tf_op jit(solution)/shard_map/dot_general | solution.py:20
  156.3 0.0 copy-done
  156.3 0.6 multiply_reduce_fusion.4
  156.9 64.3 %all-reduce = (f32[]{:T(128)}, f32[]{:T(128)}) all-reduce(f32[]{:T(128)} %get-tuple-element.3, f32[]{:T(128)} %get-tuple-element.2), channel_id=1, replica_groups=mesh['pts'=128] {'pts'}, use_global_device_ids=true, to_apply=%region_1.0 | all-reduce | flops 2 | bytes 16 | tf_op jit(solution)/shard_map/psum | solution.py:43
  222.5 0.6 multiply_reduce_fusion.3
  223.1 63.8 %psum.30 = f32[]{:T(128)} all-reduce(f32[]{:T(128)} %multiply_reduce_fusion.3), channel_id=1, replica_groups=mesh['pts'=128] {'pts'}, use_global_device_ids=true, to_apply=%region_7.0 | all-reduce | flops 1 | bytes 8 | tf_op jit(solution)/shard_map/psum | solution.py:51
  288.3 34.1 %all-gather.1 = bf16[128,1,512]{2,1,0:T(2,128)(2,1)S(1)} all-gather(bf16[1,1,512]{2,1,0:T(2,128)(2,1)S(1)} %convert.1), channel_id=1, replica_groups=mesh['pts'=128] {'pts'}, dimensions={0}, use_global_device_ids=true | all-gather | bytes 132096 | tf_op jit(solution)/shard_map/all_gather | solution.py:24
  322.4 26.6 %fusion.1 = f32[1,512]{1,0:T(1,128)S(1)} fusion(bf16[512,65536]{1,0:T(8,128)(2,1)} %exponential_convert_fusion, bf16[65536,1]{0,1:T(2,128)(2,1)S(1)} %bitcast.13), kind=kOutput, calls=%fused_computation.14 | convolution fusion | flops 67108864 | bytes 67241984 | tf_op jit(solution)/shard_map/dot_general | solution.py:20
  349.0 0.6 multiply_reduce_fusion.2
  349.6 62.1 %psum.31 = f32[]{:T(128)} all-reduce(f32[]{:T(128)} %multiply_reduce_fusion.2), channel_id=1, replica_groups=mesh['pts'=128] {'pts'}, use_global_device_ids=true, to_apply=%region_9.0 | all-reduce | flops 1 | bytes 8 | tf_op jit(solution)/shard_map/psum | solution.py:46
  413.1 0.6 multiply_subtract_fusion
  (2 shorter events, 0.0 us)
Async XLA Ops:
  7.2 80.5 %all-gather.4.cloned.1.call-start = ((), (), s32[]{:S(2)}) async-start(), calls=%async_computation | async-start | bytes 8454144 | tf_op jit(solution)/shard_map/all_gather | solution.py:10
  129.7 26.6 %copy-start = (f32[512]{0:T(512)S(1)}, f32[512]{0:T(512)}, u32[]{:S(2)}) copy-start(f32[512]{0:T(512)} %param.4) | copy-start | bytes 6148
Sparse Core Ops, SparseCore 0:
  10.8 76.7 all-gather.3
where the time goes:
time: 421 us
  blocking collectives  263 us (62%)
  matrix products  89.8 us (21%)
  waiting for transfers between devices  39.3 us (9%)
  between operations  18.7 us (4%)
  other arithmetic  9.44 us (2%)
    all_gather x2, blocking collectives, apply_operator(): lax.all_gather(direction, 'pts', axis=0, tiled=True).astype(jnp.bfloat16)  73 us
    psum x1, blocking collectives, body(): norm_now = lax.psum(jnp.sum(residual * residual), 'pts')  64.3 us
    psum x1, blocking collectives, body(): norm_next = lax.psum(jnp.sum(residual * residual), 'pts')  63.8 us
    psum x1, blocking collectives, body(): curvature = lax.psum(jnp.sum(direction * applied), 'pts')  62.1 us
    dot_general x2, matrix products, kernel_times(): return jnp.dot(kernel, coef_part, preferred_element_type=jnp.float32)  53.2 us
    all_gather x1, waiting for transfers between devices, over_all(): lax.all_gather(a, axis, axis=dim, tiled=True)  38.6 us
    dot_general x1, matrix products, kernel_times(): jnp.dot(own_points, shard_rows.T, preferred_element_type=jnp.float32)  36.6 us
  transfers between devices with their start and end apart: 1, of which 1 were waited for; matrix products, arithmetic and copies ran while one was open for 0% of the time, Pallas kernels for 0%

commit v1 on v0

v1 whole, which is shorter than its diff:
```python
import math

import jax
import jax.numpy as jnp
from jax import lax
from jax.experimental import pallas as pl
from jax.experimental.pallas import tpu as pltpu
from jax.sharding import PartitionSpec as P

f32, bf16 = jnp.float32, jnp.bfloat16
BLK, DIM = 512, 64
SCALE = math.log2(math.e) / DIM
ROWS = [(dx, dc) for dx in range(4) for dc in range(2)]
COLS = [(0, 0), (0, 1), (3, 0), (1, 1), (1, 3), (3, 2), (2, 3), (0, 2), (2, 0), (2, 2)]
FULL_COLS = range(1, 7)
SELF_COLS = [0, 7, 8, 9]
FULL_ROWS = [2, 3]
SELF_ROWS = [0, 1, 4, 5]
NR, NC = len(ROWS), len(COLS)
NFULL = 8 * 6


def position():
    me = lax.axis_index("pts")
    return me // 32, (me // 8) % 4, (me // 2) % 4, me % 2


def at_rows(dx, dc):
    z, y, x, c = position()
    return ((z * 4 + y) * 4 + (x + dx) % 4) * 2 + (c + dc) % 2


def at_cols(dz, dy):
    z, y, x, c = position()
    return (((z + dz) % 4 * 4 + (y + dy) % 4) * 4 + x) * 2 + c


def send(src, dst, ssem, rsem, dev):
    cp = pltpu.make_async_remote_copy(
        src_ref=src, dst_ref=dst, send_sem=ssem, recv_sem=rsem,
        device_id=(dev,), device_id_type=pl.DeviceIdType.MESH)
    cp.start()
    return cp


def low(v):
    return v.astype(bf16).astype(f32)


def three(v):
    hi = low(v)
    mid = low(v - hi)
    return hi, mid, low(v - hi - mid)


def put_rows(parts, first):
    row = lax.broadcasted_iota(jnp.int32, (16, BLK), 0)
    tile = jnp.where((row >= 3 - first) & (row < 6 - first), 1.0, 0.0).astype(f32)
    for k, part in enumerate(parts):
        tile = jnp.where(row == first + k, jnp.broadcast_to(part, (16, BLK)), tile)
    return tile.astype(bf16)


def build_left(raw, left):
    wide = raw.astype(f32)
    norm = -SCALE * jnp.sum(wide * wide, axis=0, keepdims=True)
    rows = put_rows(three(norm), 0)
    stack = jnp.concatenate([raw, raw, raw, rows, jnp.zeros((48, BLK), bf16)], axis=0)
    left[...] = stack.T


def build_right(raw, right):
    wide = raw.astype(f32)
    norm = -SCALE * jnp.sum(wide * wide, axis=0, keepdims=True)
    hi, mid, lo = three(wide * (2.0 * SCALE))
    right[0:64, :] = hi.astype(bf16)
    right[64:128, :] = mid.astype(bf16)
    right[128:192, :] = lo.astype(bf16)
    right[192:208, :] = put_rows(three(norm), 3)
    right[208:256, :] = jnp.zeros((48, BLK), bf16)


def half(k):
    return pl.ds(pl.multiple_of(k * 256, 256), 256)


def which_half(r, c):
    z, y, x, core = position()
    dz, dy = COLS[c]
    dx, dc = ROWS[r]
    if dz:
        return z // 2
    if dy:
        return y // 2
    if dx:
        return x // 2
    return core


def entries(left, right):
    return jnp.exp2(jnp.dot(left, right, preferred_element_type=f32)).astype(bf16)


def across(kernel, vec, first):
    wide = kernel.astype(f32)
    out = None
    for q in range(wide.shape[1] // 128):
        term = wide[:, 128 * q:128 * (q + 1)] * vec[pl.ds(first + q, 1), :]
        out = term if out is None else out + term
    return out


def fill_vectors(tile, rows_vec, cols_vec, exact):
    hi = low(tile)
    lo = low(tile - hi) if exact else jnp.zeros_like(tile)
    if cols_vec is not None:
        cols_vec[...] = tile if exact else hi
    if rows_vec is not None:
        for q in range(4):
            both = jnp.concatenate([jnp.broadcast_to(hi[q:q + 1, :], (8, 128)),
                                    jnp.broadcast_to(lo[q:q + 1, :], (8, 128))], axis=0)
            rows_vec[:, 128 * q:128 * (q + 1)] = both.astype(bf16)


def kernel(pts_ref, tgt_ref, ridge_ref, coef_ref, res_ref,
           raw_r, raw_c, left, right, kst, kdiag, t_r, t_c, y_r, y_c, vr, vc, prow, pcol,
           out_r, out_c, in1_r, in1_c, in2_r, in2_c, sc_out, sc1, sc2,
           s_raw, q_raw_r, q_raw_c, s_t, q_t_r, q_t_c, s_part, q_part, s_y, q_y_r, q_y_c,
           s_sc, q_sc):
    ridge = ridge_ref[0]
    raw_r[0] = pts_ref[...].astype(f32).T.astype(bf16)
    own_t = jnp.concatenate([tgt_ref[...], jnp.zeros((4, 128), f32)], axis=0)
    t_r[0] = own_t

    barrier = pltpu.get_barrier_semaphore()
    for r in range(1, NR):
        pl.semaphore_signal(barrier, inc=1, device_id=(at_rows(*ROWS[r]),), device_id_type=pl.DeviceIdType.MESH)
    for k in range(1, 16):
        pl.semaphore_signal(barrier, inc=1, device_id=(at_cols(k // 4, k % 4),), device_id_type=pl.DeviceIdType.MESH)
    build_left(raw_r[0], left.at[0])
    build_right(raw_r[0], right.at[0])
    pl.semaphore_wait(barrier, NR - 1 + 15)

    raws = {}
    for r in (1, 2, 6, 4):
        dx, dc = ROWS[r]
        raws[r] = send(raw_r.at[0], raw_r.at[r], s_raw.at[r], q_raw_r.at[r], at_rows(-dx, -dc))
    for c in range(1, NC):
        dz, dy = COLS[c]
        raws[NR + c] = send(raw_r.at[0], raw_c.at[c], s_raw.at[NR + c], q_raw_c.at[c], at_cols(-dz, -dy))
    ts = []
    for r in range(1, NR):
        dx, dc = ROWS[r]
        ts.append(send(t_r.at[0], t_r.at[r], s_t.at[r], q_t_r.at[r], at_rows(-dx, -dc)))
    for c in range(1, NC):
        dz, dy = COLS[c]
        ts.append(send(t_r.at[0], t_c.at[c], s_t.at[NR + c], q_t_c.at[c], at_cols(-dz, -dy)))

    for r in (2, 6, 4):
        raws[r].wait_recv()
        raws[r + 1] = send(raw_r.at[r], raw_r.at[r + 1], s_raw.at[r + 1], q_raw_r.at[r + 1], at_rows(0, 1))
        build_left(raw_r[r], left.at[r])
    for r in (1, 3, 7, 5):
        raws[r].wait_recv()
        build_left(raw_r[r], left.at[r])

    def form_full(t, r, c):
        for h in range(2):
            kst[t, 256 * h:256 * (h + 1), :] = entries(left[r, 256 * h:256 * (h + 1), :], right[c])

    def form_self(x):
        c = SELF_COLS[x]
        for i, r in enumerate(FULL_ROWS):
            form_full(NFULL + 4 * x + i, r, c)
        for j, r in enumerate(SELF_ROWS):
            t, rows = NFULL + 4 * x + 2 + j // 2, pl.ds(256 * (j % 2), 256)
            if x == 0 and j == 0:
                kdiag[...] = entries(left[0, 256:512, :], right[0, :, 256:512])
                kst[t, rows, :] = entries(left[0, 0:256, :], right[0])
            else:
                b = which_half(r, c)
                kst[t, rows, 0:256] = entries(left[r, half(b), :], right[c, :, half(b)])
                kst[t, rows, 256:512] = entries(left[r, 0:256, :], right[c, :, 256:512])

    form_self(0)

    def form_cols(c, carry):
        pltpu.make_async_copy(raw_c.at[c], raw_c.at[c], q_raw_c.at[c]).wait()
        build_right(raw_c[c], right.at[c])
        for r in range(NR):
            form_full((c - 1) * NR + r, r, c)
        return carry

    lax.fori_loop(1, 7, form_cols, 0)
    for x in (1, 2, 3):
        c = SELF_COLS[x]
        raws[NR + c].wait_recv()
        build_right(raw_c[c], right.at[c])
        form_self(x)
    for cp in raws.values():
        cp.wait_send()

    def multiply():
        for r in range(NR):
            prow[r] = jnp.zeros((BLK, 128), f32)
        for c in range(NC):
            pcol[c] = jnp.zeros((16, BLK), f32)

        def tile(t, r, c):
            for k in range(8):
                rows = pl.ds(64 * k, 64)
                prow[r, rows, :] += across(kst[t, rows, :], vc.at[c], 0)
            return jnp.dot(vr[r], kst[t], preferred_element_type=f32)

        def cols(c, carry):
            total = None
            for r in range(NR):
                part = tile((c - 1) * NR + r, r, c)
                total = part if total is None else total + part
            pcol[c] = total
            return carry

        def quad(k_ref, r, c, p, q, both):
            for k in range(4):
                rows = pl.ds(pl.multiple_of(p * 256 + 64 * k, 64), 64)
                prow[r, rows, :] += across(k_ref[64 * k:64 * (k + 1), :], vc.at[c], 2 * q)
            if both:
                pcol[c, :, half(q)] += jnp.dot(vr[r, :, half(p)], k_ref[...], preferred_element_type=f32)

        def selfs(x):
            c = SELF_COLS[x]
            total = None
            for i, r in enumerate(FULL_ROWS):
                part = tile(NFULL + 4 * x + i, r, c)
                total = part if total is None else total + part
            pcol[c] = total
            for j, r in enumerate(SELF_ROWS):
                t, rows = NFULL + 4 * x + 2 + j // 2, pl.ds(256 * (j % 2), 256)
                diag = x == 0 and j == 0
                b = 0 if diag else which_half(r, c)
                quad(kst.at[t, rows, 0:256], r, c, b, b, not diag)
                quad(kst.at[t, rows, 256:512], r, c, 0, 1, True)
            if x == 0:
                quad(kdiag, 0, 0, 1, 1, False)

        lax.fori_loop(1, 7, cols, 0)
        for x in range(4):
            selfs(x)

    def row_share(r):
        rows = [jnp.sum(prow[r, 128 * q:128 * (q + 1), :].T, axis=0, keepdims=True) for q in range(4)]
        return jnp.concatenate(rows + [jnp.zeros((4, 128), f32)], axis=0)

    def col_share(c):
        both = pcol[c, 0:1, :] + pcol[c, 8:9, :]
        rows = [both[:, 128 * q:128 * (q + 1)] for q in range(4)]
        return jnp.concatenate(rows + [jnp.zeros((4, 128), f32)], axis=0)

    def exchange(in_r, in_c):
        cps = []
        for c in range(1, NC):
            out_c[c] = col_share(c)
            cps.append(send(out_c.at[c], in_c.at[c], s_part.at[NR + c], q_part.at[NR + c], at_cols(*COLS[c])))
        for r in range(1, NR):
            out_r[r] = row_share(r)
            cps.append(send(out_r.at[r], in_r.at[r], s_part.at[r], q_part.at[r], at_rows(*ROWS[r])))
        out_r[0] = row_share(0)
        out_c[0] = col_share(0)
        return cps

    def gathered(cps, in_r, in_c):
        total = out_r[0] + out_c[0]
        for cp in cps:
            cp.wait_recv()
        for c in range(1, NC):
            total += in_c[c]
        for r in range(1, NR):
            total += in_r[r]
        for cp in cps:
            cp.wait_send()
        return total

    for r in range(1, NR):
        ts[r - 1].wait_recv()
    for c in range(1, NC):
        ts[NR - 2 + c].wait_recv()
    for r in range(NR):
        fill_vectors(t_r[r], vr.at[r], vc.at[0] if r == 0 else None, False)
    for c in range(1, NC):
        fill_vectors(t_c[c], None, vc.at[c], False)
    multiply()
    cps = exchange(in1_r, in1_c)
    for cp in ts:
        cp.wait_send()
    t_own = t_r[0]
    y_own = gathered(cps, in1_r, in1_c) + ridge * t_own
    y_r[0] = y_own

    ys = []
    for c in range(1, NC):
        dz, dy = COLS[c]
        ys.append(send(y_r.at[0], y_c.at[c], s_y.at[NR + c], q_y_c.at[c], at_cols(-dz, -dy)))
    for r in range(1, NR):
        dx, dc = ROWS[r]
        ys.append(send(y_r.at[0], y_r.at[r], s_y.at[r], q_y_r.at[r], at_rows(-dx, -dc)))

    lane_row = lax.broadcasted_iota(jnp.int32, (8, 128), 0)

    def spread(values):
        out = jnp.zeros((8, 128), f32)
        for k, value in enumerate(values):
            whole = jnp.sum(jnp.sum(value, axis=0, keepdims=True), axis=1, keepdims=True)
            out = jnp.where(lane_row == k, jnp.broadcast_to(whole, (8, 128)), out)
        return out

    def stage_one(n):
        cps = []
        for r in range(1, NR):
            dx, dc = ROWS[r]
            cps.append(send(sc_out.at[n], sc1.at[n, r], s_sc.at[n, r], q_sc.at[n, r], at_rows(-dx, -dc)))
        return cps

    def stage_two(n, cps):
        total = sc_out[n]
        for r, cp in enumerate(cps):
            cp.wait_recv()
            total += sc1[n, r + 1]
        sc_out[2 + n] = total
        more = []
        for k in range(1, 16):
            more.append(send(sc_out.at[2 + n], sc2.at[n, k], s_sc.at[n, NR + k], q_sc.at[n, NR + k],
                             at_cols(-(k // 4), -(k % 4))))
        return more

    def stage_three(n, cps, more):
        total = sc_out[2 + n]
        for k, cp in enumerate(more):
            cp.wait_recv()
            total += sc2[n, k + 1]
        for cp in cps + more:
            cp.wait_send()
        return total

    sc_out[0] = spread([t_own * t_own, t_own * y_own, y_own * y_own])
    first = stage_one(0)

    for cp in ys:
        cp.wait_recv()
    for r in range(NR):
        fill_vectors(y_r[r], vr.at[r], vc.at[0] if r == 0 else None, True)
    for c in range(1, NC):
        fill_vectors(y_c[c], None, vc.at[c], True)
    second = stage_two(0, first)
    multiply()
    cps = exchange(in2_r, in2_c)
    dot = y_own * (out_r[0] + out_c[0] + ridge * y_own)
    for r in range(1, NR):
        dot += y_r[r] * out_r[r]
    for c in range(1, NC):
        dot += y_c[c] * out_c[c]
    sc_out[1] = spread([dot])
    third = stage_one(1)
    sums = stage_three(0, first, second)
    fourth = stage_two(1, third)
    for cp in ys:
        cp.wait_send()
    w_own = gathered(cps, in2_r, in2_c) + ridge * y_own
    tt, ty, yy = sums[0:1, :], sums[1:2, :], sums[2:3, :]
    alpha = tt / ty
    next_norm = alpha * alpha * yy - tt
    beta = next_norm / tt
    yw = stage_three(1, third, fourth)[0:1, :]
    curve = (1.0 + beta) * ((1.0 + beta) * ty - 2.0 * alpha * yy) + alpha * alpha * yw
    alpha2 = next_norm / curve
    res1 = t_own - alpha * y_own
    dir2 = res1 + beta * t_own
    app2 = (1.0 + beta) * y_own - alpha * w_own
    coef_ref[...] = (alpha * t_own + alpha2 * dir2)[0:4, :]
    res_ref[...] = (res1 - alpha2 * app2)[0:4, :]


def body(points, targets, ridge_weight):
    vmem = pl.BlockSpec(memory_space=pltpu.VMEM)
    dma = pltpu.SemaphoreType.DMA
    out = jax.ShapeDtypeStruct((4, 128), f32)
    coef, res = pl.pallas_call(
        kernel,
        out_shape=(out, out),
        in_specs=[vmem, vmem, pl.BlockSpec(memory_space=pltpu.SMEM)],
        out_specs=(vmem, vmem),
        scratch_shapes=[
            pltpu.VMEM((NR, DIM, BLK), bf16), pltpu.VMEM((NC, DIM, BLK), bf16),
            pltpu.VMEM((NR, BLK, 256), bf16), pltpu.VMEM((NC, 256, BLK), bf16),
            pltpu.VMEM((NFULL + 16, BLK, BLK), bf16), pltpu.VMEM((256, 256), bf16),
            pltpu.VMEM((NR, 8, 128), f32), pltpu.VMEM((NC, 8, 128), f32),
            pltpu.VMEM((NR, 8, 128), f32), pltpu.VMEM((NC, 8, 128), f32),
            pltpu.VMEM((NR, 16, BLK), bf16), pltpu.VMEM((NC, 8, 128), f32),
            pltpu.VMEM((NR, BLK, 128), f32), pltpu.VMEM((NC, 16, BLK), f32),
            pltpu.VMEM((NR, 8, 128), f32), pltpu.VMEM((NC, 8, 128), f32),
            pltpu.VMEM((NR, 8, 128), f32), pltpu.VMEM((NC, 8, 128), f32),
            pltpu.VMEM((NR, 8, 128), f32), pltpu.VMEM((NC, 8, 128), f32),
            pltpu.VMEM((4, 8, 128), f32), pltpu.VMEM((2, NR, 8, 128), f32), pltpu.VMEM((2, 16, 8, 128), f32),
            dma((NR + NC,)), dma((NR,)), dma((NC,)),
            dma((NR + NC,)), dma((NR,)), dma((NC,)),
            dma((NR + NC,)), dma((NR + NC,)),
            dma((NR + NC,)), dma((NR,)), dma((NC,)),
            dma((2, NR + 16)), dma((2, NR + 16)),
        ],
        compiler_params=pltpu.CompilerParams(
            collective_id=0, has_side_effects=True, vmem_limit_bytes=60 * 2 ** 20),
        name="cg",
    )(points, targets.reshape(4, 128), ridge_weight.reshape(1))
    return coef.reshape(-1), res.reshape(-1)


def solution(mesh):
    in_specs = (P("pts", None), P("pts"), P())
    out_specs = (P("pts"), P("pts"))
    return jax.shard_map(body, mesh=mesh, in_specs=in_specs, out_specs=out_specs, check_vma=False)
```

time: 421 us -> 68.3 us (0.16)
  blocking collectives: 263 us -> 0 us
  matrix products: 89.8 us -> 0 us
  Pallas kernels: 0 us -> 63.3 us
  waiting for transfers between devices: 39.3 us -> 0 us
  between operations: 18.7 us -> 1.3 us
  other arithmetic: 9.44 us -> 0 us
    psum x3 -> x0, blocking collectives: 190 us -> none  [the longest x1 64.3 us: body(): norm_now = lax.psum(jnp.sum(residual * residual), 'pts')]
    dot_general x3 -> x0, matrix products: 89.8 us -> none  [the longest x2 53.2 us: kernel_times(): return jnp.dot(kernel, coef_part, preferred_element_type=jnp.float32)]
    all_gather x2 -> x0, blocking collectives: 73 us -> none  [apply_operator(): lax.all_gather(direction, 'pts', axis=0, tiled=True).astype(jnp.bfloat16)]
    pallas_call x0 -> x1, Pallas kernels: none -> 63.3 us  [body(): pl.pallas_call(kernel, out_shape=(out, out), in_specs=[vmem, vmem, pl.Blo...]
    all_gather x1 -> x0, waiting for transfers between devices: 38.6 us -> none  [over_all(): lax.all_gather(a, axis, axis=dim, tiled=True)]
    reduce_sum x5 -> x0, other arithmetic: 8.15 us -> none  [the longest x1 5.43 us: kernel_times(): shard_norms = jnp.sum(widened * widened, axis=1)]
  transfers between devices with their start and end apart: 1 -> 0, of which waited for: 1 -> 0; matrix products, arithmetic and copies ran while one was open for 0% -> 0% of each run, Pallas kernels for 0% -> 0%
where the time goes in v1:
time: 68.3 us; the launch traced here: 68.1 us
  Pallas kernels  63.3 us (93%)
  local copies, waits for them, and re-layouts  3.49 us (5%)
  between operations  1.3 us (2%)
    pallas_call x1, Pallas kernels, body(): pl.pallas_call(kernel, out_shape=(out, out), in_specs=[vmem, vmem, pl.Blo...  63.3 us
    unnamed x7, local copies, waits for them, and re-layouts  3.49 us

profile of v1, /device:TPU:1, one launch (start us, length us, event | category | flops | bytes accessed | tf_op | source)
XLA Modules:
  0.0 68.1 jit_solution(14800995836160009343)
XLA Ops:
  1.3 1.6 %copy.5.pts_ref = bf16[512,64]{1,0:T(8,128)(2,1)} copy(bf16[512,64]{0,1:T(8,128)(2,1)} %param.3) | data formatting | bytes 131072 | tf_op args[0]
  2.9 63.3 %cg.1 = (f32[4,128]{1,0:T(4,128)}, f32[4,128]{1,0:T(4,128)}) custom-call(bf16[512,64]{1,0:T(8,128)(2,1)} %copy.5.pts_ref, f32[4,128]{1,0:T(4,128)} %bitcast.5, f32[1]{0:T(128)} %bitcast.4.ridge_ref), custom_call_target="tpu_custom_call" | custom-call | tf_op jit(solution)/shard_map/cg/pallas_call | solution.py:386
  66.2 0.0 copy-start.1
  66.2 0.7 copy-done.1
  66.8 0.0 copy-start
  66.8 0.6 copy.9
  67.4 0.1 copy-done
  67.5 0.6 copy.10
Async XLA Ops:
  66.2 0.7 copy-start.1
  66.8 0.7 copy-start

commit v2 on v1

--- a/solution.py
+++ b/solution.py
@@ -128,7 +128,7 @@
            s_raw, q_raw_r, q_raw_c, s_t, q_t_r, q_t_c, s_part, q_part, s_y, q_y_r, q_y_c,
            s_sc, q_sc):
     ridge = ridge_ref[0]
-    raw_r[0] = pts_ref[...].astype(f32).T.astype(bf16)
+    raw_r[0] = pts_ref[...]
     own_t = jnp.concatenate([tgt_ref[...], jnp.zeros((4, 128), f32)], axis=0)
     t_r[0] = own_t
 
@@ -139,15 +139,25 @@
         pl.semaphore_signal(barrier, inc=1, device_id=(at_cols(k // 4, k % 4),), device_id_type=pl.DeviceIdType.MESH)
     build_left(raw_r[0], left.at[0])
     build_right(raw_r[0], right.at[0])
+    kdiag[...] = entries(left[0, 256:512, :], right[0, :, 256:512])
+    kst[NFULL + 2, 0:256, :] = entries(left[0, 0:256, :], right[0])
+    prow[...] = jnp.zeros((NR, BLK, 128), f32)
     pl.semaphore_wait(barrier, NR - 1 + 15)
 
     raws = {}
-    for r in (1, 2, 6, 4):
+    for r in (1, 2, 6):
         dx, dc = ROWS[r]
         raws[r] = send(raw_r.at[0], raw_r.at[r], s_raw.at[r], q_raw_r.at[r], at_rows(-dx, -dc))
-    for c in range(1, NC):
+
+    def send_col(c):
         dz, dy = COLS[c]
         raws[NR + c] = send(raw_r.at[0], raw_c.at[c], s_raw.at[NR + c], q_raw_c.at[c], at_cols(-dz, -dy))
+
+    for c in (1, 2):
+        send_col(c)
+    raws[4] = send(raw_r.at[0], raw_r.at[4], s_raw.at[4], q_raw_r.at[4], at_rows(-2, 0))
+    for c in range(3, NC):
+        send_col(c)
     ts = []
     for r in range(1, NR):
         dx, dc = ROWS[r]
@@ -156,96 +166,65 @@
         dz, dy = COLS[c]
         ts.append(send(t_r.at[0], t_c.at[c], s_t.at[NR + c], q_t_c.at[c], at_cols(-dz, -dy)))
 
-    for r in (2, 6, 4):
+    def take_row(r):
         raws[r].wait_recv()
-        raws[r + 1] = send(raw_r.at[r], raw_r.at[r + 1], s_raw.at[r + 1], q_raw_r.at[r + 1], at_rows(0, 1))
+        if r in (2, 6, 4):
+            raws[r + 1] = send(raw_r.at[r], raw_r.at[r + 1], s_raw.at[r + 1], q_raw_r.at[r + 1], at_rows(0, 1))
         build_left(raw_r[r], left.at[r])
-    for r in (1, 3, 7, 5):
-        raws[r].wait_recv()
-        build_left(raw_r[r], left.at[r])
+
+    def take_col(c):
+        pltpu.make_async_copy(raw_c.at[c], raw_c.at[c], q_raw_c.at[c]).wait()
+        build_right(raw_c[c], right.at[c])
 
     def form_full(t, r, c):
         for h in range(2):
             kst[t, 256 * h:256 * (h + 1), :] = entries(left[r, 256 * h:256 * (h + 1), :], right[c])
+
+    def form_cols(c, rows):
+        for r in rows:
+            form_full((c - 1) * NR + r, r, c)
 
     def form_self(x):
         c = SELF_COLS[x]
         for i, r in enumerate(FULL_ROWS):
             form_full(NFULL + 4 * x + i, r, c)
         for j, r in enumerate(SELF_ROWS):
+            if x == 0 and j == 0:
+                continue
             t, rows = NFULL + 4 * x + 2 + j // 2, pl.ds(256 * (j % 2), 256)
-            if x == 0 and j == 0:
-                kdiag[...] = entries(left[0, 256:512, :], right[0, :, 256:512])
-                kst[t, rows, :] = entries(left[0, 0:256, :], right[0])
-            else:
-                b = which_half(r, c)
-                kst[t, rows, 0:256] = entries(left[r, half(b), :], right[c, :, half(b)])
-                kst[t, rows, 256:512] = entries(left[r, 0:256, :], right[c, :, 256:512])
-
+            b = which_half(r, c)
+            kst[t, rows, 0:256] = entries(left[r, half(b), :], right[c, :, half(b)])
+            kst[t, rows, 256:512] = entries(left[r, 0:256, :], right[c, :, 256:512])
+
+    near, far = (0, 1, 2, 6), (3, 7, 4, 5)
+    for r in near[1:]:
+        take_row(r)
+
+    def form_near(c, carry):
+        take_col(c)
+        form_cols(c, near)
+        return carry
+
+    def form_far(c, carry):
+        form_cols(c, far)
+        return carry
+
+    lax.fori_loop(1, 4, form_near, 0)
+    take_row(4)
+    take_row(3)
+    take_row(7)
+    lax.fori_loop(4, 5, form_near, 0)
+    take_row(5)
+    lax.fori_loop(1, 5, form_far, 0)
     form_self(0)
-
-    def form_cols(c, carry):
-        pltpu.make_async_copy(raw_c.at[c], raw_c.at[c], q_raw_c.at[c]).wait()
-        build_right(raw_c[c], right.at[c])
-        for r in range(NR):
-            form_full((c - 1) * NR + r, r, c)
-        return carry
-
-    lax.fori_loop(1, 7, form_cols, 0)
+    for c in (5, 6):
+        take_col(c)
+        form_cols(c, range(NR))
     for x in (1, 2, 3):
-        c = SELF_COLS[x]
-        raws[NR + c].wait_recv()
-        build_right(raw_c[c], right.at[c])
+        take_col(SELF_COLS[x])
         form_self(x)
     for cp in raws.values():
         cp.wait_send()
-
-    def multiply():
-        for r in range(NR):
-            prow[r] = jnp.zeros((BLK, 128), f32)
-        for c in range(NC):
-            pcol[c] = jnp.zeros((16, BLK), f32)
-
-        def tile(t, r, c):
-            for k in range(8):
-                rows = pl.ds(64 * k, 64)
-                prow[r, rows, :] += across(kst[t, rows, :], vc.at[c], 0)
-            return jnp.dot(vr[r], kst[t], preferred_element_type=f32)
-
-        def cols(c, carry):
-            total = None
-            for r in range(NR):
-                part = tile((c - 1) * NR + r, r, c)
-                total = part if total is None else total + part
-            pcol[c] = total
-            return carry
-
-        def quad(k_ref, r, c, p, q, both):
-            for k in range(4):
-                rows = pl.ds(pl.multiple_of(p * 256 + 64 * k, 64), 64)
-                prow[r, rows, :] += across(k_ref[64 * k:64 * (k + 1), :], vc.at[c], 2 * q)
-            if both:
-                pcol[c, :, half(q)] += jnp.dot(vr[r, :, half(p)], k_ref[...], preferred_element_type=f32)
-
-        def selfs(x):
-            c = SELF_COLS[x]
-            total = None
-            for i, r in enumerate(FULL_ROWS):
-                part = tile(NFULL + 4 * x + i, r, c)
-                total = part if total is None else total + part
-            pcol[c] = total
-            for j, r in enumerate(SELF_ROWS):
-                t, rows = NFULL + 4 * x + 2 + j // 2, pl.ds(256 * (j % 2), 256)
-                diag = x == 0 and j == 0
-                b = 0 if diag else which_half(r, c)
-                quad(kst.at[t, rows, 0:256], r, c, b, b, not diag)
-                quad(kst.at[t, rows, 256:512], r, c, 0, 1, True)
-            if x == 0:
-                quad(kdiag, 0, 0, 1, 1, False)
-
-        lax.fori_loop(1, 7, cols, 0)
-        for x in range(4):
-            selfs(x)
 
     def row_share(r):
         rows = [jnp.sum(prow[r, 128 * q:128 * (q + 1), :].T, axis=0, keepdims=True) for q in range(4)]
@@ -256,53 +235,126 @@
         rows = [both[:, 128 * q:128 * (q + 1)] for q in range(4)]
         return jnp.concatenate(rows + [jnp.zeros((4, 128), f32)], axis=0)
 
-    def exchange(in_r, in_c):
+    def ship(in_c, n, c, dz, dy):
+        out_c[c] = col_share(c)
+        send(out_c.at[c], in_c.at[c], s_part.at[NR + c], q_part.at[n, NR + c], at_cols(dz, dy))
+
+    def multiply(in_r, in_c, n):
+        def along(t, r, c):
+            for k in range(8):
+                rows = pl.ds(64 * k, 64)
+                prow[r, rows, :] += across(kst[t, rows, :], vc.at[c], 0)
+
+        def along_quad(k_ref, r, c, p, q):
+            for k in range(4):
+                rows = pl.ds(pl.multiple_of(p * 256 + 64 * k, 64), 64)
+                prow[r, rows, :] += across(k_ref[64 * k:64 * (k + 1), :], vc.at[c], 2 * q)
+
+        def along_self(x):
+            c = SELF_COLS[x]
+            for i, r in enumerate(FULL_ROWS):
+                along(NFULL + 4 * x + i, r, c)
+            for j, r in enumerate(SELF_ROWS):
+                t, rows = NFULL + 4 * x + 2 + j // 2, pl.ds(256 * (j % 2), 256)
+                b = 0 if x == 0 and j == 0 else which_half(r, c)
+                along_quad(kst.at[t, rows, 0:256], r, c, b, b)
+                along_quad(kst.at[t, rows, 256:512], r, c, 0, 1)
+            if x == 0:
+                along_quad(kdiag, 0, 0, 1, 1)
+
+        def down_full(base, rows, c):
+            total = None
+            for i, r in enumerate(rows):
+                part = jnp.dot(vr[r], kst[base + i], preferred_element_type=f32)
+                total = part if total is None else total + part
+            pcol[c] = total
+
+        def down(c):
+            down_full((c - 1) * NR, range(NR), c)
+
+        def down_self(x):
+            c = SELF_COLS[x]
+            down_full(NFULL + 4 * x, FULL_ROWS, c)
+            for j, r in enumerate(SELF_ROWS):
+                t, rows = NFULL + 4 * x + 2 + j // 2, pl.ds(256 * (j % 2), 256)
+                if not (x == 0 and j == 0):
+                    b = which_half(r, c)
+                    pcol[c, :, half(b)] += jnp.dot(vr[r, :, half(b)], kst[t, rows, 0:256], preferred_element_type=f32)
+                pcol[c, :, 256:512] += jnp.dot(vr[r, :, 0:256], kst[t, rows, 256:512], preferred_element_type=f32)
+
+        def vector(c):
+            if n:
+                pltpu.make_async_copy(y_c.at[c], y_c.at[c], q_y_c.at[c]).wait()
+                fill_vectors(y_c[c], None, vc.at[c], True)
+
+        for x in (3, 2, 1):
+            down_self(x)
+        along_self(0)
+        for x in (3, 2, 1):
+            ship(in_c, n, SELF_COLS[x], *COLS[SELF_COLS[x]])
+
+        def step(i, code):
+            vector(i)
+            down(7 - i)
+            for r in range(NR):
+                along((i - 1) * NR + r, r, i)
+            ship(in_c, n, 7 - i, code // 4 % 4, code % 4)
+            return code // 16
+
+        codes = sum((4 * COLS[7 - i][0] + COLS[7 - i][1]) * 16 ** (i - 1) for i in range(1, 6))
+        lax.fori_loop(1, 6, step, jnp.int32(codes))
+        for x in (1, 2, 3):
+            vector(SELF_COLS[x])
+        vector(6)
+        down(1)
+        down_self(0)
+        for x in (1, 2, 3):
+            along_self(x)
+        ship(in_c, n, 1, *COLS[1])
+        for r in (4, 5, 2, 3, 6, 7, 1, 0):
+            along(5 * NR + r, r, 6)
+            out_r[r] = row_share(r)
         cps = []
-        for c in range(1, NC):
-            out_c[c] = col_share(c)
-            cps.append(send(out_c.at[c], in_c.at[c], s_part.at[NR + c], q_part.at[NR + c], at_cols(*COLS[c])))
-        for r in range(1, NR):
-            out_r[r] = row_share(r)
-            cps.append(send(out_r.at[r], in_r.at[r], s_part.at[r], q_part.at[r], at_rows(*ROWS[r])))
-        out_r[0] = row_share(0)
+        for r in (4, 5, 2, 3, 6, 7, 1):
+            cps.append(send(out_r.at[r], in_r.at[r], s_part.at[r], q_part.at[n, r], at_rows(*ROWS[r])))
         out_c[0] = col_share(0)
         return cps
 
-    def gathered(cps, in_r, in_c):
+    def gathered(cps, in_r, in_c, n):
         total = out_r[0] + out_c[0]
+        for c in range(1, NC):
+            pltpu.make_async_copy(in_c.at[c], in_c.at[c], q_part.at[n, NR + c]).wait()
+            total += in_c[c]
         for cp in cps:
             cp.wait_recv()
-        for c in range(1, NC):
-            total += in_c[c]
         for r in range(1, NR):
             total += in_r[r]
         for cp in cps:
             cp.wait_send()
+        for c in range(1, NC):
+            pltpu.make_async_copy(out_c.at[c], out_c.at[c], s_part.at[NR + c]).wait()
         return total
 
-    for r in range(1, NR):
-        ts[r - 1].wait_recv()
-    for c in range(1, NC):
-        ts[NR - 2 + c].wait_recv()
+    for cp in ts:
+        cp.wait_recv()
     for r in range(NR):
         fill_vectors(t_r[r], vr.at[r], vc.at[0] if r == 0 else None, False)
     for c in range(1, NC):
         fill_vectors(t_c[c], None, vc.at[c], False)
-    multiply()
-    cps = exchange(in1_r, in1_c)
+    cps = multiply(in1_r, in1_c, 0)
     for cp in ts:
         cp.wait_send()
     t_own = t_r[0]
-    y_own = gathered(cps, in1_r, in1_c) + ridge * t_own
+    y_own = gathered(cps, in1_r, in1_c, 0) + ridge * t_own
     y_r[0] = y_own
 
     ys = []
+    for r in range(1, NR):
+        dx, dc = ROWS[r]
+        ys.append(send(y_r.at[0], y_r.at[r], s_y.at[r], q_y_r.at[r], at_rows(-dx, -dc)))
     for c in range(1, NC):
         dz, dy = COLS[c]
         ys.append(send(y_r.at[0], y_c.at[c], s_y.at[NR + c], q_y_c.at[c], at_cols(-dz, -dy)))
-    for r in range(1, NR):
-        dx, dc = ROWS[r]
-        ys.append(send(y_r.at[0], y_r.at[r], s_y.at[r], q_y_r.at[r], at_rows(-dx, -dc)))
 
     lane_row = lax.broadcasted_iota(jnp.int32, (8, 128), 0)
 
@@ -343,16 +395,14 @@
 
     sc_out[0] = spread([t_own * t_own, t_own * y_own, y_own * y_own])
     first = stage_one(0)
-
-    for cp in ys:
-        cp.wait_recv()
-    for r in range(NR):
-        fill_vectors(y_r[r], vr.at[r], vc.at[0] if r == 0 else None, True)
-    for c in range(1, NC):
-        fill_vectors(y_c[c], None, vc.at[c], True)
+    prow[...] = jnp.zeros((NR, BLK, 128), f32)
+
+    fill_vectors(y_own, vr.at[0], vc.at[0], True)
+    for r in range(1, NR):
+        ys[r - 1].wait_recv()
+        fill_vectors(y_r[r], vr.at[r], None, True)
     second = stage_two(0, first)
-    multiply()
-    cps = exchange(in2_r, in2_c)
+    cps = multiply(in2_r, in2_c, 1)
     dot = y_own * (out_r[0] + out_c[0] + ridge * y_own)
     for r in range(1, NR):
         dot += y_r[r] * out_r[r]
@@ -364,7 +414,7 @@
     fourth = stage_two(1, third)
     for cp in ys:
         cp.wait_send()
-    w_own = gathered(cps, in2_r, in2_c) + ridge * y_own
+    w_own = gathered(cps, in2_r, in2_c, 1) + ridge * y_own
     tt, ty, yy = sums[0:1, :], sums[1:2, :], sums[2:3, :]
     alpha = tt / ty
     next_norm = alpha * alpha * yy - tt
@@ -402,14 +452,14 @@
             pltpu.VMEM((4, 8, 128), f32), pltpu.VMEM((2, NR, 8, 128), f32), pltpu.VMEM((2, 16, 8, 128), f32),
             dma((NR + NC,)), dma((NR,)), dma((NC,)),
             dma((NR + NC,)), dma((NR,)), dma((NC,)),
-            dma((NR + NC,)), dma((NR + NC,)),
+            dma((NR + NC,)), dma((2, NR + NC)),
             dma((NR + NC,)), dma((NR,)), dma((NC,)),
             dma((2, NR + 16)), dma((2, NR + 16)),
         ],
         compiler_params=pltpu.CompilerParams(
             collective_id=0, has_side_effects=True, vmem_limit_bytes=60 * 2 ** 20),
         name="cg",
-    )(points, targets.reshape(4, 128), ridge_weight.reshape(1))
+    )(points.T, targets.reshape(4, 128), ridge_weight.reshape(1))
     return coef.reshape(-1), res.reshape(-1)
 
 

time: 68.3 us -> 70.7 us (1.035)
  Pallas kernels: 63.3 us -> 67.3 us
  local copies, waits for them, and re-layouts: 3.49 us -> 1.89 us
    pallas_call x1, Pallas kernels: 63.3 us -> 67.3 us  [body(): pl.pallas_call(kernel, out_shape=(out, out), in_specs=[vmem, vmem, pl.Blo...]
    unnamed x7 -> x6, local copies, waits for them, and re-layouts: 3.49 us -> 1.89 us
where the time goes in v2:
time: 70.7 us; the launch traced here: 70.5 us
  Pallas kernels  67.3 us (95%)
  local copies, waits for them, and re-layouts  1.89 us (3%)
  between operations  1.29 us (2%)
    pallas_call x1, Pallas kernels, body(): pl.pallas_call(kernel, out_shape=(out, out), in_specs=[vmem, vmem, pl.Blo...  67.3 us
    unnamed x6, local copies, waits for them, and re-layouts  1.89 us

profile of v2, /device:TPU:1, one launch (start us, length us, event | category | flops | bytes accessed | tf_op | source)
XLA Modules:
  0.0 70.5 jit_solution(5067773943957770530)
XLA Ops:
  1.3 67.3 %cg.1 = (f32[4,128]{1,0:T(4,128)}, f32[4,128]{1,0:T(4,128)}) custom-call(bf16[64,512]{1,0:T(8,128)(2,1)} %bitcast.6, f32[4,128]{1,0:T(4,128)} %bitcast.7, f32[1]{0:T(128)} %bitcast.5.ridge_ref), custom_call_target="tpu_custom_call" | custom-call | tf_op jit(solution)/shard_map/cg/pallas_call | solution.py:436
  68.6 0.0 copy-start.1
  68.6 0.7 copy-done.1
  69.2 0.0 copy-start
  69.2 0.6 copy.8
  69.8 0.1 copy-done
  69.9 0.6 copy.9
Async XLA Ops:
  68.6 0.7 copy-start.1
  69.2 0.7 copy-start

commit v3 on v2

v3 whole, which is shorter than its diff:
```python
import math

import jax
import jax.numpy as jnp
from jax import lax
from jax.experimental import pallas as pl
from jax.experimental.pallas import tpu as pltpu
from jax.sharding import PartitionSpec as P

f32, bf16 = jnp.float32, jnp.bfloat16
BLK, DIM = 512, 64
SCALE = math.log2(math.e) / DIM
ROWS = [(dx, dc) for dx in range(4) for dc in range(2)]
COLS = [(0, 0), (0, 1), (3, 0), (1, 1), (1, 3), (3, 2), (2, 3), (0, 2), (2, 0), (2, 2)]
FULL_COLS = range(1, 7)
SELF_COLS = [0, 7, 8, 9]
FULL_ROWS = [2, 3]
SELF_ROWS = [0, 1, 4, 5]
NR, NC = len(ROWS), len(COLS)
NFULL = 8 * 6


def position():
    me = lax.axis_index("pts")
    return me // 32, (me // 8) % 4, (me // 2) % 4, me % 2


def at_rows(dx, dc):
    z, y, x, c = position()
    return ((z * 4 + y) * 4 + (x + dx) % 4) * 2 + (c + dc) % 2


def at_cols(dz, dy):
    z, y, x, c = position()
    return (((z + dz) % 4 * 4 + (y + dy) % 4) * 4 + x) * 2 + c


def send(src, dst, ssem, rsem, dev):
    cp = pltpu.make_async_remote_copy(
        src_ref=src, dst_ref=dst, send_sem=ssem, recv_sem=rsem,
        device_id=(dev,), device_id_type=pl.DeviceIdType.MESH)
    cp.start()
    return cp


def low(v):
    return v.astype(bf16).astype(f32)


def three(v):
    hi = low(v)
    mid = low(v - hi)
    return hi, mid, low(v - hi - mid)


def put_rows(parts, first):
    row = lax.broadcasted_iota(jnp.int32, (16, BLK), 0)
    tile = jnp.where((row >= 3 - first) & (row < 6 - first), 1.0, 0.0).astype(f32)
    for k, part in enumerate(parts):
        tile = jnp.where(row == first + k, jnp.broadcast_to(part, (16, BLK)), tile)
    return tile.astype(bf16)


def build_left(raw, left):
    wide = raw.astype(f32)
    norm = -SCALE * jnp.sum(wide * wide, axis=0, keepdims=True)
    rows = put_rows(three(norm), 0)
    stack = jnp.concatenate([raw, raw, raw, rows, jnp.zeros((48, BLK), bf16)], axis=0)
    left[...] = stack.T


def build_right(raw, right):
    wide = raw.astype(f32)
    norm = -SCALE * jnp.sum(wide * wide, axis=0, keepdims=True)
    hi, mid, lo = three(wide * (2.0 * SCALE))
    right[0:64, :] = hi.astype(bf16)
    right[64:128, :] = mid.astype(bf16)
    right[128:192, :] = lo.astype(bf16)
    right[192:208, :] = put_rows(three(norm), 3)
    right[208:256, :] = jnp.zeros((48, BLK), bf16)


def half(k):
    return pl.ds(pl.multiple_of(k * 256, 256), 256)


def which_half(r, c):
    z, y, x, core = position()
    dz, dy = COLS[c]
    dx, dc = ROWS[r]
    if dz:
        return z // 2
    if dy:
        return y // 2
    if dx:
        return x // 2
    return core


def entries(left, right):
    return jnp.exp2(jnp.dot(left, right, preferred_element_type=f32)).astype(bf16)


def across(kernel, vec, first):
    wide = kernel.astype(f32)
    out = None
    for q in range(wide.shape[1] // 128):
        term = wide[:, 128 * q:128 * (q + 1)] * vec[pl.ds(first + q, 1), :]
        out = term if out is None else out + term
    return out


def fill_vectors(tile, rows_vec, cols_vec, exact):
    hi = low(tile)
    lo = low(tile - hi) if exact else jnp.zeros_like(tile)
    if cols_vec is not None:
        cols_vec[...] = tile if exact else hi
    if rows_vec is not None:
        for q in range(4):
            both = jnp.concatenate([jnp.broadcast_to(hi[q:q + 1, :], (8, 128)),
                                    jnp.broadcast_to(lo[q:q + 1, :], (8, 128))], axis=0)
            rows_vec[:, 128 * q:128 * (q + 1)] = both.astype(bf16)


def kernel(pts_ref, tgt_ref, ridge_ref, coef_ref, res_ref,
           raw_r, raw_c, left, right, kst, kdiag, t_r, t_c, y_r, y_c, vr, vc, prow, pcol,
           out_r, out_c, in_r, in_c, sc_out, sc_in,
           s_raw, q_raw_r, q_raw_c, s_t, q_t_r, q_t_c, s_part, q_part, s_y, q_y_r, q_y_c,
           s_sc, q_sc, rounds):
    ridge = ridge_ref[0]
    raw_r[0] = pts_ref[...]
    t_r[0] = jnp.concatenate([tgt_ref[...], jnp.zeros((4, 128), f32)], axis=0)

    def greet(sem):
        for dev in (at_rows(0, 1), at_rows(1, 0), at_rows(3, 0), at_cols(0, 1), at_cols(0, 3), at_cols(1, 0), at_cols(3, 0)):
            pl.semaphore_signal(sem, inc=1, device_id=(dev,), device_id_type=pl.DeviceIdType.MESH)

    barrier = pltpu.get_barrier_semaphore()
    greet(barrier)
    build_left(raw_r[0], left.at[0])
    build_right(raw_r[0], right.at[0])
    kdiag[...] = entries(left[0, 256:512, :], right[0, :, 256:512])
    kst[NFULL + 2, 0:256, :] = entries(left[0, 0:256, :], right[0])
    pl.semaphore_wait(barrier, 7)

    raws = {}

    def send_row(r):
        dx, dc = ROWS[r]
        raws[r] = send(raw_r.at[0], raw_r.at[r], s_raw.at[r], q_raw_r.at[r], at_rows(-dx, -dc))

    def send_col(c):
        dz, dy = COLS[c]
        raws[NR + c] = send(raw_r.at[0], raw_c.at[c], s_raw.at[NR + c], q_raw_c.at[c], at_cols(-dz, -dy))

    def take_row(r):
        raws[r].wait_recv()
        if r in (2, 6, 4):
            raws[r + 1] = send(raw_r.at[r], raw_r.at[r + 1], s_raw.at[r + 1], q_raw_r.at[r + 1], at_rows(0, 1))
        build_left(raw_r[r], left.at[r])

    def take_col(c):
        raws[NR + c].wait_recv()
        build_right(raw_c[c], right.at[c])

    def form_full(t, r, c):
        for h in range(2):
            kst[t, 256 * h:256 * (h + 1), :] = entries(left[r, 256 * h:256 * (h + 1), :], right[c])

    def form(cols, rows):
        for c in cols:
            for r in rows:
                form_full((c - 1) * NR + r, r, c)

    def form_self(x):
        c = SELF_COLS[x]
        for i, r in enumerate(FULL_ROWS):
            form_full(NFULL + 4 * x + i, r, c)
        for j, r in enumerate(SELF_ROWS):
            if x == 0 and j == 0:
                continue
            t, rows = NFULL + 4 * x + 2 + j // 2, pl.ds(256 * (j % 2), 256)
            b = which_half(r, c)
            kst[t, rows, 0:256] = entries(left[r, half(b), :], right[c, :, half(b)])
            kst[t, rows, 256:512] = entries(left[r, 0:256, :], right[c, :, 256:512])

    for r in (1, 2, 6):
        send_row(r)
    send_col(1)
    send_col(2)
    greet(rounds.at[0])
    prow[...] = jnp.zeros((NR, BLK, 128), f32)
    pl.semaphore_wait(rounds.at[0], 7)
    greet(rounds.at[1])
    send_row(4)
    send_col(3)
    send_col(4)
    take_row(1)
    pl.semaphore_wait(rounds.at[1], 7)
    greet(rounds.at[2])
    take_row(2)
    take_row(6)
    for c in (5, 6, 7, 8):
        send_col(c)
    take_col(1)
    form((1,), (0, 1, 2, 6))
    pl.semaphore_wait(rounds.at[2], 7)
    send_col(9)
    ts = {}
    for r in range(1, NR):
        dx, dc = ROWS[r]
        ts[r] = send(t_r.at[0], t_r.at[r], s_t.at[r], q_t_r.at[r], at_rows(-dx, -dc))
    for c in range(1, NC):
        dz, dy = COLS[c]
        ts[NR + c] = send(t_r.at[0], t_c.at[c], s_t.at[NR + c], q_t_c.at[c], at_cols(-dz, -dy))
    take_col(2)
    take_row(3)
    take_row(7)
    form((2,), (0, 1, 2, 6, 3, 7))
    form((1,), (3, 7))
    take_row(4)
    take_col(3)
    form((3,), (0, 1, 2, 6, 3, 7))
    take_row(5)
    take_col(4)
    form((4,), range(NR))
    form((1, 2, 3), (4, 5))
    form_self(0)
    for c in (5, 6):
        take_col(c)
        form((c,), range(NR))
    for x in (1, 2, 3):
        take_col(SELF_COLS[x])
        form_self(x)
    for cp in raws.values():
        cp.wait_send()

    def row_share(r):
        rows = [jnp.sum(prow[r, 128 * q:128 * (q + 1), :].T, axis=0, keepdims=True) for q in range(4)]
        return jnp.concatenate(rows + [jnp.zeros((4, 128), f32)], axis=0)

    def col_share(c):
        both = pcol[c, 0:1, :] + pcol[c, 8:9, :]
        rows = [both[:, 128 * q:128 * (q + 1)] for q in range(4)]
        return jnp.concatenate(rows + [jnp.zeros((4, 128), f32)], axis=0)

    def along_rows(t, r, c):
        for k in range(8):
            rows = pl.ds(64 * k, 64)
            prow[r, rows, :] += across(kst[t, rows, :], vc.at[c], 0)

    def along_quad(k_ref, r, c, p, q):
        for k in range(4):
            rows = pl.ds(pl.multiple_of(p * 256 + 64 * k, 64), 64)
            prow[r, rows, :] += across(k_ref[64 * k:64 * (k + 1), :], vc.at[c], 2 * q)

    def pair(r, c):
        if c in FULL_COLS:
            return (c - 1) * NR + r, None
        x = SELF_COLS.index(c)
        if r in FULL_ROWS:
            return NFULL + 4 * x + FULL_ROWS.index(r), None
        if r in SELF_ROWS:
            j = SELF_ROWS.index(r)
            return NFULL + 4 * x + 2 + j // 2, pl.ds(256 * (j % 2), 256)
        return None, None

    def along(r, c):
        t, rows = pair(r, c)
        if rows is None:
            along_rows(t, r, c)
            return
        b = 0 if r == 0 and c == 0 else which_half(r, c)
        along_quad(kst.at[t, rows, 0:256], r, c, b, b)
        along_quad(kst.at[t, rows, 256:512], r, c, 0, 1)
        if r == 0 and c == 0:
            along_quad(kdiag, 0, 0, 1, 1)

    def down(r, c, first):
        t, rows = pair(r, c)
        if rows is None:
            part = jnp.dot(vr[r], kst[t], preferred_element_type=f32)
            pcol[c] = part if first else pcol[c] + part
            return
        if not (r == 0 and c == 0):
            b = which_half(r, c)
            pcol[c, :, half(b)] += jnp.dot(vr[r, :, half(b)], kst[t, rows, 0:256], preferred_element_type=f32)
        pcol[c, :, 256:512] += jnp.dot(vr[r, :, 0:256], kst[t, rows, 256:512], preferred_element_type=f32)

    def along_list(rows, cols):
        return [(r, c) for c in cols for r in rows if pair(r, c)[0] is not None]

    def down_list(cols):
        out = []
        for c in cols:
            rows = range(NR) if c in FULL_COLS else FULL_ROWS + SELF_ROWS
            out += [(r, c, i == 0) for i, r in enumerate(rows)]
        return out

    def weave(alongs, downs):
        done = 0
        for i, item in enumerate(alongs):
            along(*item)
            upto = (i + 1) * len(downs) // len(alongs)
            for extra in downs[done:upto]:
                down(*extra)
            done = upto

    def multiply(n):
        cps = []

        def vectors(cols):
            for c in cols if n else ():
                ys[NR + c].wait_recv()
                fill_vectors(y_c[c], None, vc.at[c], True)

        def ship_cols(cols):
            for c in cols:
                out_c[c] = col_share(c)
            for c in cols:
                cps.append(send(out_c.at[c], in_c.at[n, c], s_part.at[n, NR + c], q_part.at[n, NR + c], at_cols(*COLS[c])))

        def ship_rows(rows):
            for r in rows:
                out_r[r] = row_share(r)
            for r in rows:
                cps.append(send(out_r.at[r], in_r.at[n, r], s_part.at[n, r], q_part.at[n, r], at_rows(*ROWS[r])))

        rows_a, rows_b, rows_c = (4, 5), (2, 3, 6, 7), (0, 1)
        if n:
            weave(along_list(range(NR), (0,)), [])
            vectors((1, 2))
            weave(along_list(range(NR), (1, 2)), [])
            for r in range(1, NR):
                ys[r].wait_recv()
                fill_vectors(y_r[r], vr.at[r], None, True)
            vectors((3, 4))
            weave(along_list(rows_a, (3, 4)), down_list((9,)))
            vectors((5, 6, 7, 8, 9))
            weave(along_list(rows_a, (5, 6, 7, 8, 9)), down_list((8, 7, 6)))
            ship_cols((9, 8, 7, 6))
            ship_rows(rows_a)
            weave(along_list(rows_b, range(3, NC)), down_list((5, 4, 3, 2, 1)))
            ship_cols((5, 4, 3, 2, 1))
            ship_rows(rows_b)
            weave(along_list(rows_c, range(3, NC)), down_list((0,)))
        else:
            weave(along_list(rows_a, range(NC)), down_list((9, 8, 7, 6)))
            ship_cols((9, 8, 7, 6))
            ship_rows(rows_a)
            weave(along_list(rows_b, range(NC)), down_list((5, 4, 3, 2, 1)))
            ship_cols((5, 4, 3, 2, 1))
            ship_rows(rows_b)
            weave(along_list(rows_c, range(NC)), down_list((0,)))
        out_r[1] = row_share(1)
        cps.append(send(out_r.at[1], in_r.at[n, 1], s_part.at[n, 1], q_part.at[n, 1], at_rows(*ROWS[1])))
        out_r[0] = row_share(0)
        out_c[0] = col_share(0)
        return cps

    def gathered(cps, n):
        total = out_r[0] + out_c[0]
        for cp in cps:
            cp.wait_recv()
        for c in range(1, NC):
            total += in_c[n, c]
        for r in range(1, NR):
            total += in_r[n, r]
        for cp in cps:
            cp.wait_send()
        return total

    for cp in ts.values():
        cp.wait_recv()
    for r in range(NR):
        fill_vectors(t_r[r], vr.at[r], vc.at[0] if r == 0 else None, False)
    for c in range(1, NC):
        fill_vectors(t_c[c], None, vc.at[c], False)
    cps = multiply(0)
    for cp in ts.values():
        cp.wait_send()
    t_own = t_r[0]
    y_own = gathered(cps, 0) + ridge * t_own
    y_r[0] = y_own

    ys = {}
    for r in range(1, NR):
        dx, dc = ROWS[r]
        ys[r] = send(y_r.at[0], y_r.at[r], s_y.at[r], q_y_r.at[r], at_rows(-dx, -dc))
    for c in range(1, NC):
        dz, dy = COLS[c]
        ys[NR + c] = send(y_r.at[0], y_c.at[c], s_y.at[NR + c], q_y_c.at[c], at_cols(-dz, -dy))

    lane = lax.broadcasted_iota(jnp.int32, (1, 128), 1)
    me = lax.axis_index("pts")

    def total_send(n, values):
        out = jnp.zeros((1, 128), f32)
        for k, value in enumerate(values):
            whole = jnp.sum(jnp.sum(value, axis=0, keepdims=True), axis=1, keepdims=True)
            out = jnp.where(lane == k, jnp.broadcast_to(whole, (1, 128)), out)
        sc_out[n] = out

        def one(k, carry):
            send(sc_out.at[n], sc_in.at[n, k], s_sc.at[n], q_sc.at[n], (me + k) % 128)
            return carry

        lax.fori_loop(1, 128, one, 0)

    def total_wait(n):
        every = sc_in.at[n, pl.ds(1, 127)]
        pltpu.make_async_copy(every, every, q_sc.at[n]).wait()
        out = sc_out[n] + jnp.sum(sc_in[n, 1:128], axis=0)
        pltpu.make_async_copy(every, every, s_sc.at[n]).wait()
        return out

    total_send(0, [t_own * t_own, t_own * y_own, y_own * y_own])
    prow[...] = jnp.zeros((NR, BLK, 128), f32)

    fill_vectors(y_own, vr.at[0], vc.at[0], True)
    cps = multiply(1)
    dot = y_own * (out_r[0] + out_c[0] + ridge * y_own)
    for r in range(1, NR):
        dot += y_r[r] * out_r[r]
    for c in range(1, NC):
        dot += y_c[c] * out_c[c]
    total_send(1, [dot])
    sums = total_wait(0)
    for cp in ys.values():
        cp.wait_send()
    w_own = gathered(cps, 1) + ridge * y_own
    tt, ty, yy = sums[:, 0:1], sums[:, 1:2], sums[:, 2:3]
    alpha = tt / ty
    next_norm = alpha * alpha * yy - tt
    beta = next_norm / tt
    res1 = t_own - alpha * y_own
    dir2 = res1 + beta * t_own
    app2 = (1.0 + beta) * y_own - alpha * w_own
    part = (1.0 + beta) * ((1.0 + beta) * ty - 2.0 * alpha * yy)
    alpha2 = next_norm / (part + alpha * alpha * total_wait(1)[:, 0:1])
    coef_ref[...] = (alpha * t_own + alpha2 * dir2)[0:4, :]
    res_ref[...] = (res1 - alpha2 * app2)[0:4, :]


def body(points, targets, ridge_weight):
    vmem = pl.BlockSpec(memory_space=pltpu.VMEM)
    dma = pltpu.SemaphoreType.DMA
    out = jax.ShapeDtypeStruct((4, 128), f32)
    coef, res = pl.pallas_call(
        kernel,
        out_shape=(out, out),
        in_specs=[vmem, vmem, pl.BlockSpec(memory_space=pltpu.SMEM)],
        out_specs=(vmem, vmem),
        scratch_shapes=[
            pltpu.VMEM((NR, DIM, BLK), bf16), pltpu.VMEM((NC, DIM, BLK), bf16),
            pltpu.VMEM((NR, BLK, 256), bf16), pltpu.VMEM((NC, 256, BLK), bf16),
            pltpu.VMEM((NFULL + 16, BLK, BLK), bf16), pltpu.VMEM((256, 256), bf16),
            pltpu.VMEM((NR, 8, 128), f32), pltpu.VMEM((NC, 8, 128), f32),
            pltpu.VMEM((NR, 8, 128), f32), pltpu.VMEM((NC, 8, 128), f32),
            pltpu.VMEM((NR, 16, BLK), bf16), pltpu.VMEM((NC, 8, 128), f32),
            pltpu.VMEM((NR, BLK, 128), f32), pltpu.VMEM((NC, 16, BLK), f32),
            pltpu.VMEM((NR, 8, 128), f32), pltpu.VMEM((NC, 8, 128), f32),
            pltpu.VMEM((2, NR, 8, 128), f32), pltpu.VMEM((2, NC, 8, 128), f32),
            pltpu.VMEM((2, 1, 128), f32), pltpu.VMEM((2, 128, 1, 128), f32),
            dma((NR + NC,)), dma((NR,)), dma((NC,)),
            dma((NR + NC,)), dma((NR,)), dma((NC,)),
            dma((2, NR + NC)), dma((2, NR + NC)),
            dma((NR + NC,)), dma((NR,)), dma((NC,)),
            dma((2,)), dma((2,)), pltpu.SemaphoreType.REGULAR((3,)),
        ],
        compiler_params=pltpu.CompilerParams(
            collective_id=0, has_side_effects=True, vmem_limit_bytes=60 * 2 ** 20),
        name="cg",
    )(points.T, targets.reshape(4, 128), ridge_weight.reshape(1))
    return coef.reshape(-1), res.reshape(-1)


def solution(mesh):
    in_specs = (P("pts", None), P("pts"), P())
    out_specs = (P("pts"), P("pts"))
    return jax.shard_map(body, mesh=mesh, in_specs=in_specs, out_specs=out_specs, check_vma=False)
```

time: 70.7 us -> 68.7 us (0.972)
  Pallas kernels: 67.3 us -> 65.3 us
    pallas_call x1, Pallas kernels: 67.3 us -> 65.3 us  [body(): pl.pallas_call(kernel, out_shape=(out, out), in_specs=[vmem, vmem, pl.Blo...]
where the time goes in v3:
time: 68.7 us; the launch traced here: 68.5 us
  Pallas kernels  65.3 us (95%)
  local copies, waits for them, and re-layouts  1.89 us (3%)
  between operations  1.29 us (2%)
    pallas_call x1, Pallas kernels, body(): pl.pallas_call(kernel, out_shape=(out, out), in_specs=[vmem, vmem, pl.Blo...  65.3 us
    unnamed x6, local copies, waits for them, and re-layouts  1.89 us

profile of v3, /device:TPU:1, one launch (start us, length us, event | category | flops | bytes accessed | tf_op | source)
XLA Modules:
  0.0 68.5 jit_solution(2240471468099802012)
XLA Ops:
  1.3 65.3 %cg.1 = (f32[4,128]{1,0:T(4,128)}, f32[4,128]{1,0:T(4,128)}) custom-call(bf16[64,512]{1,0:T(8,128)(2,1)} %bitcast.6, f32[4,128]{1,0:T(4,128)} %bitcast.7, f32[1]{0:T(128)} %bitcast.5.ridge_ref), custom_call_target="tpu_custom_call" | custom-call | tf_op jit(solution)/shard_map/cg/pallas_call | solution.py:449
  66.6 0.0 copy-start.1
  66.6 0.7 copy-done.1
  67.2 0.0 copy-start
  67.2 0.6 copy.8
  67.8 0.1 copy-done
  67.9 0.6 copy.9
Async XLA Ops:
  66.6 0.7 copy-start.1
  67.2 0.7 copy-start

commit v4 on v3

--- a/solution.py
+++ b/solution.py
@@ -11,7 +11,7 @@
 BLK, DIM = 512, 64
 SCALE = math.log2(math.e) / DIM
 ROWS = [(dx, dc) for dx in range(4) for dc in range(2)]
-COLS = [(0, 0), (0, 1), (3, 0), (1, 1), (1, 3), (3, 2), (2, 3), (0, 2), (2, 0), (2, 2)]
+COLS = [(0, 0), (0, 1), (1, 0), (1, 1), (3, 1), (3, 2), (2, 3), (0, 2), (2, 0), (2, 2)]
 FULL_COLS = range(1, 7)
 SELF_COLS = [0, 7, 8, 9]
 FULL_ROWS = [2, 3]
@@ -145,23 +145,36 @@
 
     raws = {}
 
-    def send_row(r):
-        dx, dc = ROWS[r]
-        raws[r] = send(raw_r.at[0], raw_r.at[r], s_raw.at[r], q_raw_r.at[r], at_rows(-dx, -dc))
-
-    def send_col(c):
-        dz, dy = COLS[c]
-        raws[NR + c] = send(raw_r.at[0], raw_c.at[c], s_raw.at[NR + c], q_raw_c.at[c], at_cols(-dz, -dy))
+    def pass_row(r, src, dx, dc):
+        raws[r] = send(raw_r.at[src], raw_r.at[r], s_raw.at[r], q_raw_r.at[r], at_rows(dx, dc))
+
+    def pass_col(c, src, dz, dy):
+        raws[NR + c] = send(src, raw_c.at[c], s_raw.at[NR + c], q_raw_c.at[c], at_cols(dz, dy))
 
     def take_row(r):
         raws[r].wait_recv()
         if r in (2, 6, 4):
-            raws[r + 1] = send(raw_r.at[r], raw_r.at[r + 1], s_raw.at[r + 1], q_raw_r.at[r + 1], at_rows(0, 1))
+            pass_row(r + 1, r, 0, 1)
         build_left(raw_r[r], left.at[r])
 
     def take_col(c):
         raws[NR + c].wait_recv()
+        if c == 1:
+            pass_col(3, raw_c.at[1], 3, 0)
+            pass_col(4, raw_c.at[1], 1, 0)
+            pass_col(7, raw_c.at[1], 0, 3)
+        if c == 2:
+            pass_col(8, raw_c.at[2], 3, 0)
+        if c == 7:
+            pass_col(5, raw_c.at[7], 1, 0)
+        if c == 8:
+            pass_col(6, raw_c.at[8], 0, 1)
+        if c == 6:
+            pass_col(9, raw_c.at[6], 0, 1)
         build_right(raw_c[c], right.at[c])
+
+    def fence():
+        pl.delay(1)
 
     def form_full(t, r, c):
         for h in range(2):
@@ -184,28 +197,52 @@
             kst[t, rows, 0:256] = entries(left[r, half(b), :], right[c, :, half(b)])
             kst[t, rows, 256:512] = entries(left[r, 0:256, :], right[c, :, 256:512])
 
-    for r in (1, 2, 6):
-        send_row(r)
-    send_col(1)
-    send_col(2)
+    core = lax.axis_index("pts") % 2
+    pass_row(2, 0, 3, 0)
+    pass_row(6, 0, 1, 0)
+    pass_col(1, raw_r.at[0], 0, 3)
+    pass_col(2, raw_r.at[0], 3, 0)
+    pass_row(1, 0, 0, 1)
     greet(rounds.at[0])
     prow[...] = jnp.zeros((NR, BLK, 128), f32)
+    take_row(1)
+    take_row(2)
+    take_row(6)
+    pass_row(4, 2 + 4 * core, 3 + 2 * core, 0)
+    take_col(1)
+    take_col(2)
+    fence()
+    form((1,), (0, 1, 2, 6))
+    fence()
     pl.semaphore_wait(rounds.at[0], 7)
     greet(rounds.at[1])
-    send_row(4)
-    send_col(3)
-    send_col(4)
-    take_row(1)
+    take_row(3)
+    take_row(7)
+    fence()
+    form((2,), (0, 1, 2, 6, 3, 7))
+    form((1,), (3, 7))
+    fence()
+    take_row(4)
+    take_col(7)
+    take_col(8)
+    take_col(3)
+    take_col(4)
+    fence()
+    form((3,), (0, 1, 2, 6, 3, 7))
+    fence()
     pl.semaphore_wait(rounds.at[1], 7)
     greet(rounds.at[2])
-    take_row(2)
-    take_row(6)
-    for c in (5, 6, 7, 8):
-        send_col(c)
-    take_col(1)
-    form((1,), (0, 1, 2, 6))
+    take_row(5)
+    fence()
+    form((4,), range(NR))
+    fence()
+    take_col(6)
+    take_col(5)
+    fence()
+    form((1, 2, 3), (4, 5))
+    form_self(0)
+    fence()
     pl.semaphore_wait(rounds.at[2], 7)
-    send_col(9)
     ts = {}
     for r in range(1, NR):
         dx, dc = ROWS[r]
@@ -213,25 +250,17 @@
     for c in range(1, NC):
         dz, dy = COLS[c]
         ts[NR + c] = send(t_r.at[0], t_c.at[c], s_t.at[NR + c], q_t_c.at[c], at_cols(-dz, -dy))
-    take_col(2)
-    take_row(3)
-    take_row(7)
-    form((2,), (0, 1, 2, 6, 3, 7))
-    form((1,), (3, 7))
-    take_row(4)
-    take_col(3)
-    form((3,), (0, 1, 2, 6, 3, 7))
-    take_row(5)
-    take_col(4)
-    form((4,), range(NR))
-    form((1, 2, 3), (4, 5))
-    form_self(0)
-    for c in (5, 6):
-        take_col(c)
-        form((c,), range(NR))
-    for x in (1, 2, 3):
-        take_col(SELF_COLS[x])
-        form_self(x)
+    fence()
+    form_self(1)
+    form_self(2)
+    fence()
+    form((5,), range(NR))
+    fence()
+    form((6,), range(NR))
+    fence()
+    take_col(9)
+    form_self(3)
+    fence()
     for cp in raws.values():
         cp.wait_send()
 
@@ -328,30 +357,48 @@
 
         rows_a, rows_b, rows_c = (4, 5), (2, 3, 6, 7), (0, 1)
         if n:
+            fence()
             weave(along_list(range(NR), (0,)), [])
+            fence()
             vectors((1, 2))
+            fence()
             weave(along_list(range(NR), (1, 2)), [])
+            fence()
             for r in range(1, NR):
                 ys[r].wait_recv()
                 fill_vectors(y_r[r], vr.at[r], None, True)
             vectors((3, 4))
+            fence()
             weave(along_list(rows_a, (3, 4)), down_list((9,)))
+            fence()
             vectors((5, 6, 7, 8, 9))
-            weave(along_list(rows_a, (5, 6, 7, 8, 9)), down_list((8, 7, 6)))
-            ship_cols((9, 8, 7, 6))
+            fence()
+            weave(along_list(rows_a, (5, 6, 7, 8, 9)), down_list((5, 6, 7)))
+            fence()
+            ship_cols((9, 5, 6, 7))
             ship_rows(rows_a)
-            weave(along_list(rows_b, range(3, NC)), down_list((5, 4, 3, 2, 1)))
-            ship_cols((5, 4, 3, 2, 1))
+            fence()
+            weave(along_list(rows_b, range(3, NC)), down_list((8, 3, 4, 2, 1)))
+            fence()
+            ship_cols((8, 3, 4, 2, 1))
             ship_rows(rows_b)
+            fence()
             weave(along_list(rows_c, range(3, NC)), down_list((0,)))
+            fence()
         else:
-            weave(along_list(rows_a, range(NC)), down_list((9, 8, 7, 6)))
-            ship_cols((9, 8, 7, 6))
+            fence()
+            weave(along_list(rows_a, range(NC)), down_list((9, 5, 6, 7)))
+            fence()
+            ship_cols((9, 5, 6, 7))
             ship_rows(rows_a)
-            weave(along_list(rows_b, range(NC)), down_list((5, 4, 3, 2, 1)))
-            ship_cols((5, 4, 3, 2, 1))
+            fence()
+            weave(along_list(rows_b, range(NC)), down_list((8, 3, 4, 2, 1)))
+            fence()
+            ship_cols((8, 3, 4, 2, 1))
             ship_rows(rows_b)
+            fence()
             weave(along_list(rows_c, range(NC)), down_list((0,)))
+            fence()
         out_r[1] = row_share(1)
         cps.append(send(out_r.at[1], in_r.at[n, 1], s_part.at[n, 1], q_part.at[n, 1], at_rows(*ROWS[1])))
         out_r[0] = row_share(0)
@@ -405,7 +452,14 @@
             send(sc_out.at[n], sc_in.at[n, k], s_sc.at[n], q_sc.at[n], (me + k) % 128)
             return carry
 
-        lax.fori_loop(1, 128, one, 0)
+        def some(i, carry):
+            for j in range(16):
+                one(16 * i + j + 1, carry)
+            return carry
+
+        lax.fori_loop(0, 7, some, 0)
+        for k in range(113, 128):
+            one(k, 0)
 
     def total_wait(n):
         every = sc_in.at[n, pl.ds(1, 127)]

time: 68.7 us -> 60.1 us (0.87)
  Pallas kernels: 65.3 us -> 56.7 us
    pallas_call x1, Pallas kernels: 65.3 us -> 56.7 us  [body(): pl.pallas_call(kernel, out_shape=(out, out), in_specs=[vmem, vmem, pl.Blo...]
where the time goes in v4:
time: 60.1 us; the launch traced here: 59.9 us
  Pallas kernels  56.7 us (94%)
  local copies, waits for them, and re-layouts  1.89 us (3%)
  between operations  1.29 us (2%)
    pallas_call x1, Pallas kernels, body(): pl.pallas_call(kernel, out_shape=(out, out), in_specs=[vmem, vmem, pl.Blo...  56.7 us
    unnamed x6, local copies, waits for them, and re-layouts  1.89 us

profile of v4, /device:TPU:1, one launch (start us, length us, event | category | flops | bytes accessed | tf_op | source)
XLA Modules:
  0.0 59.9 jit_solution(17015100900657580059)
XLA Ops:
  1.3 56.7 %cg.1 = (f32[4,128]{1,0:T(4,128)}, f32[4,128]{1,0:T(4,128)}) custom-call(bf16[64,512]{1,0:T(8,128)(2,1)} %bitcast.6, f32[4,128]{1,0:T(4,128)} %bitcast.7, f32[1]{0:T(128)} %bitcast.5.ridge_ref), custom_call_target="tpu_custom_call" | custom-call | tf_op jit(solution)/shard_map/cg/pallas_call | solution.py:503
  57.9 0.0 copy-start.1
  58.0 0.7 %copy-done.1 = f32[4,128]{1,0:T(4,128)S(1)} copy-done((f32[4,128]{1,0:T(4,128)S(1)}, f32[4,128]{1,0:T(4,128)}, u32[]{:S(2)}) %copy-start.1) | copy-done | bytes 2072
  58.6 0.0 copy-start
  58.6 0.6 copy.8
  59.2 0.1 copy-done
  59.3 0.6 copy.9
Async XLA Ops:
  57.9 0.7 %copy-start.1 = (f32[4,128]{1,0:T(4,128)S(1)}, f32[4,128]{1,0:T(4,128)}, u32[]{:S(2)}) copy-start(f32[4,128]{1,0:T(4,128)} %get-tuple-element.4) | copy-start | bytes 6148
  58.6 0.7 %copy-start = (f32[4,128]{1,0:T(4,128)S(1)}, f32[4,128]{1,0:T(4,128)}, u32[]{:S(2)}) copy-start(f32[4,128]{1,0:T(4,128)} %get-tuple-element.5) | copy-start | bytes 6148
